TPU v7x, 32 devices: a whole 2x2x4 slice. The times are simulated.
32 devices in a mesh: bank: 4 (over z), lane: 4 (over y, core), site: 2 (over x).
Axes of the slice: x: 2, y: 2, z: 4, core: 2. Of those that a mesh axis runs over, the one named last changes fastest.
Arguments:
- wave_parts: float32 [4, 64, 128, 128], P('site', ('bank', 'lane')), parts along dimension 0, may hold values from -6 to 6
- level_table: float32 [128, 128, 128], P(('site', 'bank', 'lane')), parts along dimension 0, may hold values from -2 to 2
- phase_angles: float32 [4, 128], P('site'), parts along dimension 0, may hold values from 0.3 to 1.2
- mix_angles: float32 [4, 4], P('site'), parts along dimension 0, may hold values from 0.3 to 1.2
Outputs:
- final_parts: float32 [4, 64, 128, 128], P('site', ('bank', 'lane')), parts along dimension 0
There are 2 independent parts, one for each index of `site`. A program takes and returns all parts, laid end to end along the dimension named above; each array names one. Nothing has to cross between parts.
All inputs are finite; a program needn't handle non-finite values.
Results may differ from a plain program's by a relative error of at most 0.0003.
Values sent between devices are 32-bit elements; how exact they have to be, the bound alone decides.
A program may use at most 64 MiB of HBM per device.

v0:
```python
import jax
import jax.numpy as jnp
from jax import lax
from jax.sharding import PartitionSpec as P

LAYERS = 2


def partner(value, axis, distance):
    return lax.ppermute(value, axis, [(i, i ^ 1 << distance) for i in range(lax.axis_size(axis))])


def count_bits(values, count):
    places = jnp.arange(count.bit_length() - 1, dtype=jnp.int32)
    return jnp.sum(values[..., None] >> places & 1, axis=-1)


def plane_table(count, angle):
    rank = jnp.arange(count, dtype=jnp.int32)
    apart = count_bits(rank[:, None] ^ rank[None, :], count)
    minus = count_bits(rank[:, None] & (rank[:, None] ^ rank[None, :]), count)
    bits = count.bit_length() - 1
    size = jnp.cos(angle) ** (bits - apart).astype(jnp.float32) * jnp.sin(angle) ** apart.astype(
        jnp.float32
    )
    return size * jnp.where(minus % 2 == 1, -1.0, 1.0).astype(jnp.float32)


def apply_along(values, dim, angle):
    real_part = plane_table(values.shape[dim], angle)
    moved = jnp.tensordot(values, real_part, axes=([dim], [0]), precision=lax.Precision.HIGHEST)
    return jnp.moveaxis(moved, -1, dim)


def turn_phase(values, levels, angle):
    turn = angle * levels
    return jnp.stack(
        [
            values[0] * jnp.cos(turn) + values[1] * jnp.sin(turn),
            values[1] * jnp.cos(turn) - values[0] * jnp.sin(turn),
        ]
    )


def local(wave_parts, level_table, phase_angles, mix_angles):
    values = wave_parts
    for layer in range(LAYERS):
        values = turn_phase(values, level_table, phase_angles[layer])
        values = apply_along(values, 3, mix_angles[layer, 0])
        values = apply_along(values, 2, mix_angles[layer, 1])
        values = apply_along(values, 1, mix_angles[layer, 2])
        for bit in range(lax.axis_size("bank").bit_length() - 1):
            other = partner(values, "bank", bit)
            sign = 1.0 - 2.0 * (lax.axis_index("bank") >> bit & 1).astype(jnp.float32)
            angle = mix_angles[layer, 2]
            real_new = jnp.cos(angle) * values[0] - sign * jnp.sin(angle) * other[0]
            imag_new = jnp.cos(angle) * values[1] - sign * jnp.sin(angle) * other[1]
            values = jnp.stack([real_new, imag_new])
        for bit in range(lax.axis_size("lane").bit_length() - 1):
            other = partner(values, "lane", bit)
            sign = 1.0 - 2.0 * (lax.axis_index("lane") >> bit & 1).astype(jnp.float32)
            angle = mix_angles[layer, 3]
            real_new = jnp.cos(angle) * values[0] - sign * jnp.sin(angle) * other[0]
            imag_new = jnp.cos(angle) * values[1] - sign * jnp.sin(angle) * other[1]
            values = jnp.stack([real_new, imag_new])
    return values


def solution(mesh):
    placed = (
        P("site", ("bank", "lane"), None, None),
        P(("site", "bank", "lane"), None, None),
        P("site", None),
        P("site", None),
    )
    return jax.shard_map(
        local,
        mesh=mesh,
        in_specs=placed,
        out_specs=P("site", ("bank", "lane"), None, None),
        check_vma=False,
    )
```

profile of v0, /device:TPU:0, one launch (start us, length us, event | category | flops | bytes accessed | tf_op | source)
XLA Modules:
  0.0 130.0 jit_solution(11545531451258868033)
XLA Ops:
  0.0 0.0 copy-start
  0.0 1.6 %fusion.137 = (f32[1,1]{1,0:T(1,128)}, f32[1,1]{1,0:T(1,128)}, f32[1,1]{1,0:T(1,128)}, f32[1,1]{1,0:T(1,128)}, f32[1,1]{1,0:T(1,128)}, /*index=5*/f32[1,1]{1,0:T(1,128)}, f32[1,1]{1,0:T(1,128)}, f32[1,1]{1,0:T(1,128)}) fusion(f32[2,4]{1,0:T(2,128)} %param.7), kind=kLoop, calls=%fused_computation.190 | loop fusion | bytes 64 | tf_op jit(solution)/shard_map/slice | solution.py:62
  5.8 0.8 slice_bitcast_fusion.1
  6.7 0.0 copy-done
  6.7 2.0 %fusion.27 = (f32[1,4,128,128]{3,2,1,0:T(8,128)S(1)}, f32[1,4,128,128]{3,2,1,0:T(8,128)S(1)}) fusion(f32[2,4,128,128]{3,2,1,0:T(8,128)} %param.4, f32[4,128,128]{2,1,0:T(8,128)S(1)} %copy-done, f32[128]{0:T(128)S(1)} %get-tuple-element.31), kind=kLoop, calls=%fused_computation.61 | loop fusion | flops 458752 | bytes 1311232 | tf_op jit(solution)/shard_map/stack | solution.py:37
  8.7 0.8 fusion
  9.4 1.1 fusion.37
  10.5 0.2 copy.13
  10.8 1.1 convolution_bitcast_fusion.1
  11.8 3.1 %collective-permute-start = (f32[2,4,128,128]{3,1,2,0:T(4,128)S(1)}, f32[2,4,128,128]{3,1,2,0:T(4,128)S(1)}, u32[]{:S(2)}, u32[]{:S(2)}) collective-permute-start(f32[2,4,128,128]{3,1,2,0:T(4,128)S(1)} %convolution_bitcast_fusion.1), channel_id=1, source_target_pairs={{0,8},{8,0},{16,24},{24,16},{1,9},{9,1},{17,25},{25,17},{2,10},{10... | collective-permute-start | bytes 1572872 | tf_op jit(solution)/shard_map/ppermute | solution.py:10
  15.0 11.9 %collective-permute-done = f32[2,4,128,128]{3,1,2,0:T(4,128)S(1)} collective-permute-done((f32[2,4,128,128]{3,1,2,0:T(4,128)S(1)}, f32[2,4,128,128]{3,1,2,0:T(4,128)S(1)}, u32[]{:S(2)}, u32[]{:S(2)}) %collective-permute-start) | collective-permute-done | bytes 524320 | tf_op jit(solution)/shard_map/ppermute | solution.py:10
  26.9 0.1 fusion.25
  27.0 0.1 pad_maximum_fusion
  27.2 2.8 %collective-permute-start.1 = (f32[2,4,128,128]{3,1,2,0:T(4,128)S(1)}, f32[2,4,128,128]{3,1,2,0:T(4,128)S(1)}, u32[]{:S(2)}, u32[]{:S(2)}) collective-permute-start(f32[2,4,128,128]{3,1,2,0:T(4,128)S(1)} %pad_maximum_fusion), channel_id=1, source_target_pairs={{0,16},{8,24},{16,0},{24,8},{1,17},{9,25},{17,1},{25,9},{2,18},{10... | collective-permute-start | bytes 1572872 | tf_op jit(solution)/shard_map/ppermute | solution.py:10
  30.0 22.5 %collective-permute-done.1 = f32[2,4,128,128]{3,1,2,0:T(4,128)S(1)} collective-permute-done((f32[2,4,128,128]{3,1,2,0:T(4,128)S(1)}, f32[2,4,128,128]{3,1,2,0:T(4,128)S(1)}, u32[]{:S(2)}, u32[]{:S(2)}) %collective-permute-start.1) | collective-permute-done | bytes 524320 | tf_op jit(solution)/shard_map/ppermute | solution.py:10
  52.4 0.1 fusion.23
  52.6 0.1 pad_maximum_fusion.1
  52.7 0.1 collective-permute-start.2
  54.2 0.5 collective-permute-done.2
  54.7 0.1 fusion.21
  54.8 0.1 pad_maximum_fusion.2
  54.9 1.5 %collective-permute-start.3 = (f32[2,4,128,128]{3,1,2,0:T(4,128)S(1)}, f32[2,4,128,128]{3,1,2,0:T(4,128)S(1)}, u32[]{:S(2)}, u32[]{:S(2)}) collective-permute-start(f32[2,4,128,128]{3,1,2,0:T(4,128)S(1)} %pad_maximum_fusion.2), channel_id=1, source_target_pairs={{0,4},{2,6},{4,0},{6,2},{1,5},{3,7},{5,1},{7,3},{8,12},{10,14},{12... | collective-permute-start | bytes 1572872 | tf_op jit(solution)/shard_map/ppermute | solution.py:10
  60.6 8.3 %collective-permute-done.3 = f32[2,4,128,128]{3,1,2,0:T(4,128)S(1)} collective-permute-done((f32[2,4,128,128]{3,1,2,0:T(4,128)S(1)}, f32[2,4,128,128]{3,1,2,0:T(4,128)S(1)}, u32[]{:S(2)}, u32[]{:S(2)}) %collective-permute-start.3) | collective-permute-done | bytes 524320 | tf_op jit(solution)/shard_map/ppermute | solution.py:10
  69.0 2.2 %add_bitcast_fusion = (f32[1,4,128,128]{3,1,2,0:T(4,128)S(1)}, f32[1,4,128,128]{3,1,2,0:T(4,128)S(1)}) fusion(f32[4,128,128]{2,1,0:T(8,128)S(1)} %copy-done, f32[128]{0:T(128)S(1)} %get-tuple-element.32, f32[2,4,128,128]{3,1,2,0:T(4,128)S(1)} %collective-permute-done.3, f32[]{:T(128)S(6)} %mul.409, f32[1,4,128,128]{3,1,2,0:T(4,128)S(1)} %get-tuple-element.19, ...), kind=kLoop, calls=%fused_computation.68 | loop fusion | flops 851968 | bytes 1835528 | tf_op jit(solution)/shard_map/stack | solution.py:37
  71.2 0.1 pad_maximum_fusion.3
  71.3 0.8 fusion.6
  72.1 1.1 fusion.42
  73.2 0.2 copy.18
  73.4 1.1 convolution_bitcast_fusion
  74.5 0.6 collective-permute-start.4
  75.1 12.6 %collective-permute-done.4 = f32[2,4,128,128]{3,1,2,0:T(4,128)S(1)} collective-permute-done((f32[2,4,128,128]{3,1,2,0:T(4,128)S(1)}, f32[2,4,128,128]{3,1,2,0:T(4,128)S(1)}, u32[]{:S(2)}, u32[]{:S(2)}) %collective-permute-start.4) | collective-permute-done | bytes 524320 | tf_op jit(solution)/shard_map/ppermute | solution.py:10
  87.6 0.1 fusion.15
  87.8 0.1 pad_maximum_fusion.4
  87.9 2.3 %collective-permute-start.5 = (f32[2,4,128,128]{3,1,2,0:T(4,128)S(1)}, f32[2,4,128,128]{3,1,2,0:T(4,128)S(1)}, u32[]{:S(2)}, u32[]{:S(2)}) collective-permute-start(f32[2,4,128,128]{3,1,2,0:T(4,128)S(1)} %pad_maximum_fusion.4), channel_id=1, source_target_pairs={{0,16},{8,24},{16,0},{24,8},{1,17},{9,25},{17,1},{25,9},{2,18},{10... | collective-permute-start | bytes 1572872 | tf_op jit(solution)/shard_map/ppermute | solution.py:10
  90.1 22.2 %collective-permute-done.5 = f32[2,4,128,128]{3,1,2,0:T(4,128)S(1)} collective-permute-done((f32[2,4,128,128]{3,1,2,0:T(4,128)S(1)}, f32[2,4,128,128]{3,1,2,0:T(4,128)S(1)}, u32[]{:S(2)}, u32[]{:S(2)}) %collective-permute-start.5) | collective-permute-done | bytes 524320 | tf_op jit(solution)/shard_map/ppermute | solution.py:10
  112.3 0.1 fusion.13
  112.5 0.1 pad_maximum_fusion.5
  112.6 0.1 collective-permute-start.6
  114.1 0.5 collective-permute-done.6
  114.6 0.1 fusion.11
  114.7 0.1 pad_maximum_fusion.6
  114.8 1.5 %collective-permute-start.7 = (f32[2,4,128,128]{3,1,2,0:T(4,128)S(1)}, f32[2,4,128,128]{3,1,2,0:T(4,128)S(1)}, u32[]{:S(2)}, u32[]{:S(2)}) collective-permute-start(f32[2,4,128,128]{3,1,2,0:T(4,128)S(1)} %pad_maximum_fusion.6), channel_id=1, source_target_pairs={{0,4},{2,6},{4,0},{6,2},{1,5},{3,7},{5,1},{7,3},{8,12},{10,14},{12... | collective-permute-start | bytes 1572872 | tf_op jit(solution)/shard_map/ppermute | solution.py:10
  116.3 12.6 %collective-permute-done.7 = f32[2,4,128,128]{3,1,2,0:T(4,128)S(1)} collective-permute-done((f32[2,4,128,128]{3,1,2,0:T(4,128)S(1)}, f32[2,4,128,128]{3,1,2,0:T(4,128)S(1)}, u32[]{:S(2)}, u32[]{:S(2)}) %collective-permute-start.7) | collective-permute-done | bytes 524320 | tf_op jit(solution)/shard_map/ppermute | solution.py:10
  128.9 0.1 fusion.9
  129.0 0.1 pad_maximum_fusion.7
  129.1 0.8 copy.10
  (8 shorter events, 0.2 us)
Async XLA Ops:
  0.0 6.7 %copy-start = (f32[4,128,128]{2,1,0:T(8,128)S(1)}, f32[4,128,128]{2,1,0:T(8,128)}, u32[]{:S(2)}) copy-start(f32[4,128,128]{2,1,0:T(8,128)} %param.5) | copy-start | bytes 786436
  11.8 15.0 %collective-permute-start = (f32[2,4,128,128]{3,1,2,0:T(4,128)S(1)}, f32[2,4,128,128]{3,1,2,0:T(4,128)S(1)}, u32[]{:S(2)}, u32[]{:S(2)}) collective-permute-start(f32[2,4,128,128]{3,1,2,0:T(4,128)S(1)} %convolution_bitcast_fusion.1), channel_id=1, source_target_pairs={{0,8},{8,0},{16,24},{24,16},{1,9},{9,1},{17,25},{25,17},{2,10},{10... | collective-permute-start | bytes 1572872 | tf_op jit(solution)/shard_map/ppermute | solution.py:10
  27.2 25.3 %collective-permute-start.1 = (f32[2,4,128,128]{3,1,2,0:T(4,128)S(1)}, f32[2,4,128,128]{3,1,2,0:T(4,128)S(1)}, u32[]{:S(2)}, u32[]{:S(2)}) collective-permute-start(f32[2,4,128,128]{3,1,2,0:T(4,128)S(1)} %pad_maximum_fusion), channel_id=1, source_target_pairs={{0,16},{8,24},{16,0},{24,8},{1,17},{9,25},{17,1},{25,9},{2,18},{10... | collective-permute-start | bytes 1572872 | tf_op jit(solution)/shard_map/ppermute | solution.py:10
  52.7 2.0 %collective-permute-start.2 = (f32[2,4,128,128]{3,1,2,0:T(4,128)S(1)}, f32[2,4,128,128]{3,1,2,0:T(4,128)S(1)}, u32[]{:S(2)}, u32[]{:S(2)}) collective-permute-start(f32[2,4,128,128]{3,1,2,0:T(4,128)S(1)} %pad_maximum_fusion.1), channel_id=1, source_target_pairs={{0,2},{2,0},{4,6},{6,4},{1,3},{3,1},{5,7},{7,5},{8,10},{10,8},{12,... | collective-permute-start | bytes 1572872 | tf_op jit(solution)/shard_map/ppermute | solution.py:10
  54.9 14.0 %collective-permute-start.3 = (f32[2,4,128,128]{3,1,2,0:T(4,128)S(1)}, f32[2,4,128,128]{3,1,2,0:T(4,128)S(1)}, u32[]{:S(2)}, u32[]{:S(2)}) collective-permute-start(f32[2,4,128,128]{3,1,2,0:T(4,128)S(1)} %pad_maximum_fusion.2), channel_id=1, source_target_pairs={{0,4},{2,6},{4,0},{6,2},{1,5},{3,7},{5,1},{7,3},{8,12},{10,14},{12... | collective-permute-start | bytes 1572872 | tf_op jit(solution)/shard_map/ppermute | solution.py:10
  74.5 13.2 %collective-permute-start.4 = (f32[2,4,128,128]{3,1,2,0:T(4,128)S(1)}, f32[2,4,128,128]{3,1,2,0:T(4,128)S(1)}, u32[]{:S(2)}, u32[]{:S(2)}) collective-permute-start(f32[2,4,128,128]{3,1,2,0:T(4,128)S(1)} %convolution_bitcast_fusion), channel_id=1, source_target_pairs={{0,8},{8,0},{16,24},{24,16},{1,9},{9,1},{17,25},{25,17},{2,10},{10... | collective-permute-start | bytes 1572872 | tf_op jit(solution)/shard_map/ppermute | solution.py:10
  87.9 24.5 %collective-permute-start.5 = (f32[2,4,128,128]{3,1,2,0:T(4,128)S(1)}, f32[2,4,128,128]{3,1,2,0:T(4,128)S(1)}, u32[]{:S(2)}, u32[]{:S(2)}) collective-permute-start(f32[2,4,128,128]{3,1,2,0:T(4,128)S(1)} %pad_maximum_fusion.4), channel_id=1, source_target_pairs={{0,16},{8,24},{16,0},{24,8},{1,17},{9,25},{17,1},{25,9},{2,18},{10... | collective-permute-start | bytes 1572872 | tf_op jit(solution)/shard_map/ppermute | solution.py:10
  112.6 2.0 %collective-permute-start.6 = (f32[2,4,128,128]{3,1,2,0:T(4,128)S(1)}, f32[2,4,128,128]{3,1,2,0:T(4,128)S(1)}, u32[]{:S(2)}, u32[]{:S(2)}) collective-permute-start(f32[2,4,128,128]{3,1,2,0:T(4,128)S(1)} %pad_maximum_fusion.5), channel_id=1, source_target_pairs={{0,2},{2,0},{4,6},{6,4},{1,3},{3,1},{5,7},{7,5},{8,10},{10,8},{12,... | collective-permute-start | bytes 1572872 | tf_op jit(solution)/shard_map/ppermute | solution.py:10
  114.8 14.0 %collective-permute-start.7 = (f32[2,4,128,128]{3,1,2,0:T(4,128)S(1)}, f32[2,4,128,128]{3,1,2,0:T(4,128)S(1)}, u32[]{:S(2)}, u32[]{:S(2)}) collective-permute-start(f32[2,4,128,128]{3,1,2,0:T(4,128)S(1)} %pad_maximum_fusion.6), channel_id=1, source_target_pairs={{0,4},{2,6},{4,0},{6,2},{1,5},{3,7},{5,1},{7,3},{8,12},{10,14},{12... | collective-permute-start | bytes 1572872 | tf_op jit(solution)/shard_map/ppermute | solution.py:10
where the time goes:
time: 130 us
  waiting for transfers between devices  91 us (70%)
  starting transfers between devices  11.9 us (9%)
  between operations  11.4 us (9%)
  other arithmetic  6.24 us (5%)
  matrix products  5.78 us (4%)
  local copies, waits for them, and re-layouts  3.68 us (3%)
    ppermute x8, waiting for transfers between devices, partner(): lax.ppermute(value, axis, [(i, i ^ 1 << distance) for i in range(lax.axis...  91 us
    ppermute x8, starting transfers between devices, partner(): lax.ppermute(value, axis, [(i, i ^ 1 << distance) for i in range(lax.axis...  11.9 us
    dot_general x6, matrix products, apply_along(): jnp.tensordot(values, real_part, axes=([dim], [0]), precision=lax.Precisi...  5.78 us
    another operation x3, other arithmetic, turn_phase(): jnp.stack([values[0] * jnp.cos(turn) + values[1] * jnp.sin(turn), values[...  4.3 us
  transfers between devices with their start and end apart: 8, of which 8 were waited for; matrix products, arithmetic and copies ran while one was open for 0% of the time, Pallas kernels for 0%

commit v1 on v0

v1 whole, which is shorter than its diff:
```python
import functools

import jax
import jax.numpy as jnp
from jax import lax
from jax.experimental import pallas as pl
from jax.experimental.pallas import tpu as pltpu
from jax.sharding import PartitionSpec as P

SUB = 8
MESH = pl.DeviceIdType.MESH


def sin_cos(turn):
    h = 0.5 * turn
    q = h * h
    s = -1.0 / 39916800 + q * (1.0 / 6227020800)
    for term in (1.0 / 362880, -1.0 / 5040, 1.0 / 120, -1.0 / 6, 1.0):
        s = term + q * s
    s = h * s
    c = -1.0 / 3628800 + q * (1.0 / 479001600)
    for term in (1.0 / 40320, -1.0 / 720, 1.0 / 24, -0.5, 1.0):
        c = term + q * c
    return 2.0 * s * c, 1.0 - 2.0 * s * s


def rotate_bits(x, count, sc):
    s, c = sc
    shape = x.shape
    step = 1
    while step < count:
        y = x.reshape(count // (2 * step), 2, step, *shape[1:])
        u, v = y[:, 0], y[:, 1]
        x = jnp.stack([c * u - s * v, c * v + s * u], axis=1).reshape(shape)
        step *= 2
    return x


def rotate_sublanes(x, sc):
    s, c = sc
    place = lax.broadcasted_iota(jnp.int32, s.shape, 0)
    step = 1
    while step < SUB:
        upper = (place // step) % 2 == 1
        down = pltpu.roll(x, step, 1)
        if 2 * step == SUB:
            x = c * x + jnp.where(upper, s, -s) * down
        else:
            up = pltpu.roll(x, SUB - step, 1)
            x = c * x + jnp.where(upper, s, -s) * jnp.where(upper, down, up)
        step *= 2
    return x


def lane_table(sc, lanes):
    s = jnp.broadcast_to(sc[0][0:1], (lanes, lanes))
    c = jnp.broadcast_to(sc[1][0:1], (lanes, lanes))
    i = lax.broadcasted_iota(jnp.int32, (lanes, lanes), 0)
    j = lax.broadcasted_iota(jnp.int32, (lanes, lanes), 1)
    table = jnp.ones((lanes, lanes), jnp.float32)
    step = 1
    while step < lanes:
        a, b = (i // step) % 2, (j // step) % 2
        table = table * jnp.where(a == b, c, jnp.where(a > b, -s, s))
        step *= 2
    high = table.astype(jnp.bfloat16)
    low = (table - high.astype(jnp.float32)).astype(jnp.bfloat16)
    top = jnp.concatenate([high, low], axis=1)
    bottom = jnp.concatenate([high, jnp.zeros_like(low)], axis=1)
    return jnp.concatenate([top, bottom], axis=0)


def rotate_lanes(x, table):
    lanes = x.shape[1]
    high = x.astype(jnp.bfloat16)
    low = (x - high.astype(jnp.float32)).astype(jnp.bfloat16)
    out = jnp.dot(
        jnp.concatenate([high, low], axis=1), table, preferred_element_type=jnp.float32
    )
    return out[:, :lanes] + out[:, lanes:]


def kernel(
    n_bank, n_lane, chunks,
    wave_hbm, level_hbm, phase_ref, mix_ref, out_ref,
    wave, level, mixed, send, recv, level_recv, turned, back,
    in_sem, level_send_sem, level_recv_sem, send_sem, recv_sem, turn_sem, back_sem,
):
    n = n_bank * n_lane
    bank, lane = lax.axis_index("bank"), lax.axis_index("lane")
    me = bank * n_lane + lane
    _, blocks, rows, lanes = wave.shape
    tiles = rows // SUB
    units = blocks * tiles // n
    each = units // chunks

    peers = []
    order = [n_bank // 2] + [k for k in range(n_bank) if k != n_bank // 2]
    for kb in order:
        for kl in range(n_lane):
            if kb or kl:
                pb, pn = lax.rem(bank + kb, n_bank), lax.rem(lane + kl, n_lane)
                peers.append(({"bank": pb, "lane": pn}, pb * n_lane + pn))

    barrier = pltpu.get_barrier_semaphore()
    for device, _ in peers:
        pl.semaphore_signal(barrier, inc=1, device_id=device, device_id_type=MESH)
    load_wave = pltpu.make_async_copy(wave_hbm, wave, in_sem.at[0])
    load_level = pltpu.make_async_copy(level_hbm, level, in_sem.at[1])
    load_level.start()
    load_wave.start()

    sc = [[sin_cos(jnp.full((SUB, lanes), mix_ref[y, g], jnp.float32)) for g in range(4)] for y in range(2)]
    tables = [lane_table(sc[y][0], lanes) for y in range(2)]

    load_level.wait()
    load_wave.wait()
    for block in range(blocks):
        here = level[block * tiles : (block + 1) * tiles].reshape(rows, lanes)
        s, c = sin_cos(phase_ref[0:1, :] * here)
        real, imag = wave[0, block], wave[1, block]
        x = jnp.concatenate([real * c + imag * s, imag * c - real * s], axis=0)
        x = rotate_lanes(x, tables[0])
        x = rotate_sublanes(x.reshape(2 * tiles, SUB, lanes), sc[0][1])
        x = x.reshape(2, tiles, SUB, lanes)
        for part in range(2):
            mixed[part, block] = rotate_bits(x[part], tiles, sc[0][1])

    pl.semaphore_wait(barrier, n - 1)
    for device, there in peers:
        pltpu.make_async_remote_copy(
            src_ref=level_units(level, there, units),
            dst_ref=level_recv.at[me],
            send_sem=level_send_sem,
            recv_sem=level_recv_sem,
            device_id=device,
            device_id_type=MESH,
        ).start()
    level_recv[me] = level_units(level, me, units)[...]

    for part in range(2):
        x = rotate_bits(mixed[part], blocks, sc[0][2])
        x = x.reshape(n, chunks, each, SUB, lanes)
        for k in range(chunks):
            send[k, :, part] = x[:, k]
    for k in range(chunks):
        for device, there in peers:
            pltpu.make_async_remote_copy(
                src_ref=send.at[k, there],
                dst_ref=recv.at[k, me],
                send_sem=send_sem.at[k],
                recv_sem=recv_sem.at[k],
                device_id=device,
                device_id_type=MESH,
            ).start()
        recv[k, me] = send[k, me]

    def wait_all(buffer, sem):
        whole = buffer.at[pl.ds(0, n - 1)]
        pltpu.make_async_copy(whole, whole, sem).wait()

    wait_all(level_recv, level_recv_sem)
    for k in range(chunks):
        wait_all(recv.at[k], recv_sem.at[k])
        x = recv[k].reshape(n_bank, n_lane, 2, each, SUB, lanes)
        x = rotate_bits(x, n_bank, sc[0][2])
        x = jnp.stack([rotate_bits(x[b], n_lane, sc[0][3]) for b in range(n_bank)])
        x = x.reshape(n, 2, each, SUB, lanes)
        s, c = sin_cos(phase_ref[1:2, :] * level_recv[:, k * each : (k + 1) * each])
        real, imag = x[:, 0], x[:, 1]
        x = jnp.stack([real * c + imag * s, imag * c - real * s], axis=1)
        x = rotate_lanes(x.reshape(n * 2 * each * SUB, lanes), tables[1])
        x = rotate_sublanes(x.reshape(n * 2 * each, SUB, lanes), sc[1][1])
        x = x.reshape(n_bank, n_lane, 2, each, SUB, lanes)
        x = rotate_bits(x, n_bank, sc[1][2])
        x = jnp.stack([rotate_bits(x[b], n_lane, sc[1][3]) for b in range(n_bank)])
        turned[k] = x.reshape(n, 2, each, SUB, lanes)
        for device, there in peers:
            pltpu.make_async_remote_copy(
                src_ref=turned.at[k, there],
                dst_ref=back.at[k, me],
                send_sem=turn_sem.at[k],
                recv_sem=back_sem.at[k],
                device_id=device,
                device_id_type=MESH,
            ).start()
        back[k, me] = turned[k, me]

    for k in range(chunks):
        wait_all(back.at[k], back_sem.at[k])
    for part in range(2):
        x = jnp.stack([back[k, :, part] for k in range(chunks)], axis=1)
        x = x.reshape(blocks, tiles, SUB, lanes)
        x = rotate_bits(x, blocks, sc[1][2])
        for block in range(blocks):
            out_ref[part, block] = rotate_bits(x[block], tiles, sc[1][1]).reshape(rows, lanes)

    wait_all(level_recv, level_send_sem)
    for k in range(chunks):
        wait_all(recv.at[k], send_sem.at[k])
        wait_all(back.at[k], turn_sem.at[k])


def level_units(level, there, units):
    return level.at[pl.ds(there * units, units)]


def local(n_bank, n_lane, wave_parts, level_table, phase_angles, mix_angles):
    parts, blocks, rows, lanes = wave_parts.shape
    n = n_bank * n_lane
    tiles = rows // SUB
    units = blocks * tiles // n
    chunks = min(4, units)
    each = units // chunks
    exchange = pltpu.VMEM((chunks, n, 2, each, SUB, lanes), jnp.float32)
    dma = pltpu.SemaphoreType.DMA
    return pl.pallas_call(
        functools.partial(kernel, n_bank, n_lane, chunks),
        out_shape=jax.ShapeDtypeStruct(wave_parts.shape, jnp.float32),
        in_specs=[
            pl.BlockSpec(memory_space=pl.ANY),
            pl.BlockSpec(memory_space=pl.ANY),
            pl.BlockSpec(memory_space=pltpu.VMEM),
            pl.BlockSpec(memory_space=pltpu.SMEM),
        ],
        out_specs=pl.BlockSpec(memory_space=pltpu.VMEM),
        scratch_shapes=[
            pltpu.VMEM(wave_parts.shape, jnp.float32),
            pltpu.VMEM((blocks * tiles, SUB, lanes), jnp.float32),
            pltpu.VMEM((2, blocks, tiles, SUB, lanes), jnp.float32),
            exchange,
            exchange,
            pltpu.VMEM((n, units, SUB, lanes), jnp.float32),
            exchange,
            exchange,
            dma((2,)),
            dma,
            dma,
            dma((chunks,)),
            dma((chunks,)),
            dma((chunks,)),
            dma((chunks,)),
        ],
        compiler_params=pltpu.CompilerParams(
            collective_id=0, has_side_effects=True, vmem_limit_bytes=48 * 1024 * 1024
        ),
    )(wave_parts, level_table.reshape(blocks * tiles, SUB, lanes), phase_angles, mix_angles)


def solution(mesh):
    placed = (
        P("site", ("bank", "lane"), None, None),
        P(("site", "bank", "lane"), None, None),
        P("site", None),
        P("site", None),
    )
    return jax.shard_map(
        functools.partial(local, mesh.shape["bank"], mesh.shape["lane"]),
        mesh=mesh,
        in_specs=placed,
        out_specs=P("site", ("bank", "lane"), None, None),
        check_vma=False,
    )
```

time: 130 us -> 40.8 us (0.31)
  waiting for transfers between devices: 91 us -> 0 us
  Pallas kernels: 0 us -> 36.4 us
  starting transfers between devices: 11.9 us -> 0 us
  between operations: 11.4 us -> 0.01 us
  other arithmetic: 6.24 us -> 0 us
  matrix products: 5.78 us -> 0 us
    ppermute x8 -> x0, waiting for transfers between devices: 91 us -> none  [partner(): lax.ppermute(value, axis, [(i, i ^ 1 << distance) for i in range(lax.axis...]
    pallas_call x0 -> x1, Pallas kernels: none -> 36.4 us  [local(): pl.pallas_call(functools.partial(kernel, n_bank, n_lane, chunks), out_sha...]
    ppermute x8 -> x0, starting transfers between devices: 11.9 us -> none  [partner(): lax.ppermute(value, axis, [(i, i ^ 1 << distance) for i in range(lax.axis...]
    dot_general x6 -> x0, matrix products: 5.78 us -> none  [apply_along(): jnp.tensordot(values, real_part, axes=([dim], [0]), precision=lax.Precisi...]
    another operation x10 -> x0, other arithmetic: 5.11 us -> none  [the longest x3 4.3 us: turn_phase(): jnp.stack([values[0] * jnp.cos(turn) + values[1] * jnp.sin(turn), values[...]
    unnamed x2 -> x9, local copies, waits for them, and re-layouts: 0.01 us -> 4.14 us
    slice x1 -> x0, local copies, waits for them, and re-layouts: 1.63 us -> none  [local(): angle = mix_angles[layer, 3]]
  transfers between devices with their start and end apart: 8 -> 0, of which waited for: 8 -> 0; matrix products, arithmetic and copies ran while one was open for 0% -> 0% of each run, Pallas kernels for 0% -> 0%
where the time goes in v1:
time: 40.8 us; the launch traced here: 40.6 us
  Pallas kernels  36.4 us (89%)
  local copies, waits for them, and re-layouts  4.14 us (10%)
    pallas_call x1, Pallas kernels, local(): pl.pallas_call(functools.partial(kernel, n_bank, n_lane, chunks), out_sha...  36.4 us
    unnamed x9, local copies, waits for them, and re-layouts  4.14 us

profile of v1, /device:TPU:0, one launch (start us, length us, event | category | flops | bytes accessed | tf_op | source)
XLA Modules:
  0.0 40.6 jit_solution(8245432644602611359)
XLA Ops:
  0.0 0.0 copy-start.2
  0.0 0.7 %copy-done.2 = f32[2,128]{1,0:T(2,128)S(1)} copy-done((f32[2,128]{1,0:T(2,128)S(1)}, f32[2,128]{1,0:T(2,128)}, u32[]{:S(2)}) %copy-start.2) | copy-done | bytes 1048
  0.7 0.0 copy-start
  0.7 1.0 %copy-done = f32[2,4,128,128]{3,2,1,0:T(8,128)S(1)} copy-done((f32[2,4,128,128]{3,2,1,0:T(8,128)S(1)}, f32[2,4,128,128]{3,2,1,0:T(8,128)}, u32[]{:S(2)}) %copy-start) | copy-done | bytes 524312
  1.7 0.0 copy-start.1
  1.7 0.9 %copy-done.1 = f32[4,128,128]{2,1,0:T(8,128)S(1)} copy-done((f32[4,128,128]{2,1,0:T(8,128)S(1)}, f32[4,128,128]{2,1,0:T(8,128)}, u32[]{:S(2)}) %copy-start.1) | copy-done | bytes 262168
  2.7 0.0 copy-start.3
  2.7 0.7 %copy-done.3 = f32[2,4]{1,0:T(2,128)S(1)} copy-done((f32[2,4]{1,0:T(2,128)S(1)}, f32[2,4]{1,0:T(2,128)}, u32[]{:S(2)}) %copy-start.3) | copy-done | bytes 56
  3.4 36.4 %shard_map.46 = f32[2,4,128,128]{3,2,1,0:T(8,128)S(1)} custom-call(f32[2,4,128,128]{3,2,1,0:T(8,128)S(1)} %copy-done, f32[64,8,128]{2,1,0:T(8,128)S(1)} %bitcast.1, f32[2,128]{1,0:T(2,128)S(1)} %copy-done.2, f32[2,4]{1,0:T(2,128)S(1)} %copy-done.3), custom_call_target="tpu_custom_call" | custom-call | tf_op jit(solution)/shard_map/pallas_call | solution.py:217
  39.8 0.8 %copy.6 = f32[2,4,128,128]{3,2,1,0:T(8,128)} copy(f32[2,4,128,128]{3,2,1,0:T(8,128)S(1)} %shard_map.46) | data formatting | bytes 1048576
Async XLA Ops:
  0.0 0.7 %copy-start.2 = (f32[2,128]{1,0:T(2,128)S(1)}, f32[2,128]{1,0:T(2,128)}, u32[]{:S(2)}) copy-start(f32[2,128]{1,0:T(2,128)} %phase_ref.1) | copy-start | bytes 3076
  0.7 1.0 %copy-start = (f32[2,4,128,128]{3,2,1,0:T(8,128)S(1)}, f32[2,4,128,128]{3,2,1,0:T(8,128)}, u32[]{:S(2)}) copy-start(f32[2,4,128,128]{3,2,1,0:T(8,128)} %wave_hbm.1) | copy-start | bytes 1572868
  1.7 0.9 %copy-start.1 = (f32[4,128,128]{2,1,0:T(8,128)S(1)}, f32[4,128,128]{2,1,0:T(8,128)}, u32[]{:S(2)}) copy-start(f32[4,128,128]{2,1,0:T(8,128)} %param.5) | copy-start | bytes 786436
  2.7 0.7 %copy-start.3 = (f32[2,4]{1,0:T(2,128)S(1)}, f32[2,4]{1,0:T(2,128)}, u32[]{:S(2)}) copy-start(f32[2,4]{1,0:T(2,128)} %mix_ref.1) | copy-start | bytes 100

commit v2 on v1

--- a/solution.py
+++ b/solution.py
@@ -36,6 +36,26 @@
     return x
 
 
+def rotate_list(items, sc):
+    s, c = sc
+    step = 1
+    while step < len(items):
+        items = [
+            c * x - s * items[i + step] if (i // step) % 2 == 0 else c * x + s * items[i - step]
+            for i, x in enumerate(items)
+        ]
+        step *= 2
+    return items
+
+
+def differ(index, apart, count):
+    out, bit = 0, 1
+    while bit < count:
+        out = out + lax.rem(index // bit + (apart // bit) % 2, 2) * bit
+        bit *= 2
+    return out
+
+
 def rotate_sublanes(x, sc):
     s, c = sc
     place = lax.broadcasted_iota(jnp.int32, s.shape, 0)
@@ -82,8 +102,8 @@
 
 def kernel(
     n_bank, n_lane, chunks,
-    wave_hbm, level_hbm, phase_ref, mix_ref, out_ref,
-    wave, level, mixed, send, recv, level_recv, turned, back,
+    wave_hbm, level_hbm, phase_hbm, mix_hbm, out_ref,
+    wave, level, phase_ref, mix_ref, mixed, send, recv, level_recv, turned, back, last,
     in_sem, level_send_sem, level_recv_sem, send_sem, recv_sem, turn_sem, back_sem,
 ):
     n = n_bank * n_lane
@@ -95,37 +115,30 @@
     each = units // chunks
 
     peers = []
-    order = [n_bank // 2] + [k for k in range(n_bank) if k != n_bank // 2]
-    for kb in order:
-        for kl in range(n_lane):
+    for kb in range(n_bank - 1, -1, -1):
+        for kl in range(n_lane - 1, -1, -1):
             if kb or kl:
-                pb, pn = lax.rem(bank + kb, n_bank), lax.rem(lane + kl, n_lane)
+                pb, pn = differ(bank, kb, n_bank), differ(lane, kl, n_lane)
                 peers.append(({"bank": pb, "lane": pn}, pb * n_lane + pn))
 
     barrier = pltpu.get_barrier_semaphore()
     for device, _ in peers:
         pl.semaphore_signal(barrier, inc=1, device_id=device, device_id_type=MESH)
-    load_wave = pltpu.make_async_copy(wave_hbm, wave, in_sem.at[0])
-    load_level = pltpu.make_async_copy(level_hbm, level, in_sem.at[1])
-    load_level.start()
-    load_wave.start()
-
+    loads = [
+        pltpu.make_async_copy(there, here, in_sem.at[i])
+        for i, (there, here) in enumerate(
+            [(mix_hbm, mix_ref), (level_hbm, level), (phase_hbm, phase_ref), (wave_hbm, wave)]
+        )
+    ]
+    for load in loads:
+        load.start()
+
+    loads[0].wait()
     sc = [[sin_cos(jnp.full((SUB, lanes), mix_ref[y, g], jnp.float32)) for g in range(4)] for y in range(2)]
     tables = [lane_table(sc[y][0], lanes) for y in range(2)]
 
-    load_level.wait()
-    load_wave.wait()
-    for block in range(blocks):
-        here = level[block * tiles : (block + 1) * tiles].reshape(rows, lanes)
-        s, c = sin_cos(phase_ref[0:1, :] * here)
-        real, imag = wave[0, block], wave[1, block]
-        x = jnp.concatenate([real * c + imag * s, imag * c - real * s], axis=0)
-        x = rotate_lanes(x, tables[0])
-        x = rotate_sublanes(x.reshape(2 * tiles, SUB, lanes), sc[0][1])
-        x = x.reshape(2, tiles, SUB, lanes)
-        for part in range(2):
-            mixed[part, block] = rotate_bits(x[part], tiles, sc[0][1])
-
+    for load in loads[1:]:
+        load.wait()
     pl.semaphore_wait(barrier, n - 1)
     for device, there in peers:
         pltpu.make_async_remote_copy(
@@ -137,6 +150,17 @@
             device_id_type=MESH,
         ).start()
     level_recv[me] = level_units(level, me, units)[...]
+
+    for block in range(blocks):
+        here = level[block * tiles : (block + 1) * tiles].reshape(rows, lanes)
+        s, c = sin_cos(phase_ref[0:1, :] * here)
+        real, imag = wave[0, block], wave[1, block]
+        x = jnp.concatenate([real * c + imag * s, imag * c - real * s], axis=0)
+        x = rotate_lanes(x, tables[0])
+        x = rotate_sublanes(x.reshape(2 * tiles, SUB, lanes), sc[0][1])
+        x = x.reshape(2, tiles, SUB, lanes)
+        for part in range(2):
+            mixed[part, block] = rotate_bits(x[part], tiles, sc[0][1])
 
     for part in range(2):
         x = rotate_bits(mixed[part], blocks, sc[0][2])
@@ -186,14 +210,19 @@
             ).start()
         back[k, me] = turned[k, me]
 
+    high = tiles // units
     for k in range(chunks):
         wait_all(back.at[k], back_sem.at[k])
+        x = back[k].reshape(blocks, high, 2, each, SUB, lanes)
+        x = rotate_bits(x, blocks, sc[1][2])
+        x = jnp.stack([rotate_bits(x[b], high, sc[1][1]) for b in range(blocks)])
+        last[k] = x.reshape(n, 2, each, SUB, lanes)
     for part in range(2):
-        x = jnp.stack([back[k, :, part] for k in range(chunks)], axis=1)
-        x = x.reshape(blocks, tiles, SUB, lanes)
-        x = rotate_bits(x, blocks, sc[1][2])
         for block in range(blocks):
-            out_ref[part, block] = rotate_bits(x[block], tiles, sc[1][1]).reshape(rows, lanes)
+            these = pl.ds(block * high, high)
+            items = [last[u // each, these, part, u % each] for u in range(units)]
+            x = jnp.stack(rotate_list(items, sc[1][1]), axis=1)
+            out_ref[part, block] = x.reshape(rows, lanes)
 
     wait_all(level_recv, level_send_sem)
     for k in range(chunks):
@@ -218,22 +247,25 @@
         functools.partial(kernel, n_bank, n_lane, chunks),
         out_shape=jax.ShapeDtypeStruct(wave_parts.shape, jnp.float32),
         in_specs=[
-            pl.BlockSpec(memory_space=pl.ANY),
-            pl.BlockSpec(memory_space=pl.ANY),
-            pl.BlockSpec(memory_space=pltpu.VMEM),
-            pl.BlockSpec(memory_space=pltpu.SMEM),
+            pl.BlockSpec(memory_space=pltpu.HBM),
+            pl.BlockSpec(memory_space=pltpu.HBM),
+            pl.BlockSpec(memory_space=pltpu.HBM),
+            pl.BlockSpec(memory_space=pltpu.HBM),
         ],
         out_specs=pl.BlockSpec(memory_space=pltpu.VMEM),
         scratch_shapes=[
             pltpu.VMEM(wave_parts.shape, jnp.float32),
             pltpu.VMEM((blocks * tiles, SUB, lanes), jnp.float32),
+            pltpu.VMEM(phase_angles.shape, jnp.float32),
+            pltpu.SMEM(mix_angles.shape, jnp.float32),
             pltpu.VMEM((2, blocks, tiles, SUB, lanes), jnp.float32),
             exchange,
             exchange,
             pltpu.VMEM((n, units, SUB, lanes), jnp.float32),
             exchange,
             exchange,
-            dma((2,)),
+            exchange,
+            dma((4,)),
             dma,
             dma,
             dma((chunks,)),
@@ -242,7 +274,7 @@
             dma((chunks,)),
         ],
         compiler_params=pltpu.CompilerParams(
-            collective_id=0, has_side_effects=True, vmem_limit_bytes=48 * 1024 * 1024
+            collective_id=0, has_side_effects=True, vmem_limit_bytes=67043328
         ),
     )(wave_parts, level_table.reshape(blocks * tiles, SUB, lanes), phase_angles, mix_angles)
 

time: 40.8 us -> 38.9 us (0.953)
  local copies, waits for them, and re-layouts: 4.14 us -> 1.87 us
    unnamed x9 -> x1, local copies, waits for them, and re-layouts: 4.14 us -> 1.87 us
where the time goes in v2:
time: 38.9 us; the launch traced here: 38.7 us
  Pallas kernels  36.8 us (95%)
  local copies, waits for them, and re-layouts  1.87 us (5%)
    pallas_call x1, Pallas kernels, local(): pl.pallas_call(functools.partial(kernel, n_bank, n_lane, chunks), out_sha...  36.8 us
    unnamed x1, local copies, waits for them, and re-layouts  1.87 us

profile of v2, /device:TPU:0, one launch (start us, length us, event | category | flops | bytes accessed | tf_op | source)
XLA Modules:
  0.0 38.7 jit_solution(5609582928446860369)
XLA Ops:
  0.0 36.8 %shard_map.46 = f32[2,4,128,128]{3,2,1,0:T(8,128)} custom-call(f32[2,4,128,128]{3,2,1,0:T(8,128)} %wave_hbm.1, f32[64,8,128]{2,1,0:T(8,128)} %bitcast.1, f32[2,128]{1,0:T(2,128)} %phase_hbm.1, f32[2,4]{1,0:T(2,128)} %mix_hbm.1), custom_call_target="tpu_custom_call" | custom-call | tf_op jit(solution)/shard_map/pallas_call | solution.py:246
  36.8 1.9 %copy.6 = f32[2,4,128,128]{3,2,1,0:T(8,128)} copy(f32[2,4,128,128]{3,2,1,0:T(8,128)} %shard_map.46) | data formatting | bytes 1048576

commit v3 on v2

--- a/solution.py
+++ b/solution.py
@@ -241,6 +241,12 @@
     units = blocks * tiles // n
     chunks = min(4, units)
     each = units // chunks
+    operands = [
+        wave_parts,
+        level_table.reshape(blocks * tiles, SUB, lanes),
+        phase_angles,
+        mix_angles,
+    ]
     exchange = pltpu.VMEM((chunks, n, 2, each, SUB, lanes), jnp.float32)
     dma = pltpu.SemaphoreType.DMA
     return pl.pallas_call(
@@ -274,9 +280,9 @@
             dma((chunks,)),
         ],
         compiler_params=pltpu.CompilerParams(
-            collective_id=0, has_side_effects=True, vmem_limit_bytes=67043328
+            collective_id=0, has_side_effects=True, vmem_limit_bytes=40 * 1024 * 1024
         ),
-    )(wave_parts, level_table.reshape(blocks * tiles, SUB, lanes), phase_angles, mix_angles)
+    )(*[pltpu.with_memory_space_constraint(value, pltpu.HBM) for value in operands])
 
 
 def solution(mesh):

time: 38.9 us -> 37 us (0.951)
  local copies, waits for them, and re-layouts: 1.87 us -> 0.8 us
  Pallas kernels: 36.8 us -> 36 us
    unnamed x1, local copies, waits for them, and re-layouts: 1.87 us -> 0.8 us
    pallas_call x1, Pallas kernels: 36.8 us -> 36 us  [local(): pl.pallas_call(functools.partial(kernel, n_bank, n_lane, chunks), out_sha...]
where the time goes in v3:
time: 37 us; the launch traced here: 36.8 us
  Pallas kernels  36 us (97%)
  local copies, waits for them, and re-layouts  0.8 us (2%)
    pallas_call x1, Pallas kernels, local(): pl.pallas_call(functools.partial(kernel, n_bank, n_lane, chunks), out_sha...  36 us
    unnamed x1, local copies, waits for them, and re-layouts  0.8 us

profile of v3, /device:TPU:0, one launch (start us, length us, event | category | flops | bytes accessed | tf_op | source)
XLA Modules:
  0.0 36.8 jit_solution(753261413549805241)
XLA Ops:
  0.0 36.0 %shard_map.46 = f32[2,4,128,128]{3,2,1,0:T(8,128)S(1)} custom-call(f32[2,4,128,128]{3,2,1,0:T(8,128)} %wave_hbm.1, f32[64,8,128]{2,1,0:T(8,128)} %bitcast.1, f32[2,128]{1,0:T(2,128)} %phase_hbm.1, f32[2,4]{1,0:T(2,128)} %mix_hbm.1), custom_call_target="tpu_custom_call" | custom-call | tf_op jit(solution)/shard_map/pallas_call | solution.py:252
  36.0 0.8 %copy.6 = f32[2,4,128,128]{3,2,1,0:T(8,128)} copy(f32[2,4,128,128]{3,2,1,0:T(8,128)S(1)} %shard_map.46) | data formatting | bytes 1048576

commit v4 on v3

--- a/solution.py
+++ b/solution.py
@@ -115,14 +115,14 @@
     each = units // chunks
 
     peers = []
-    for kb in range(n_bank - 1, -1, -1):
-        for kl in range(n_lane - 1, -1, -1):
+    for kb in range(n_bank):
+        for kl in range(n_lane):
             if kb or kl:
                 pb, pn = differ(bank, kb, n_bank), differ(lane, kl, n_lane)
                 peers.append(({"bank": pb, "lane": pn}, pb * n_lane + pn))
 
     barrier = pltpu.get_barrier_semaphore()
-    for device, _ in peers:
+    for device, _ in reversed(peers):
         pl.semaphore_signal(barrier, inc=1, device_id=device, device_id_type=MESH)
     loads = [
         pltpu.make_async_copy(there, here, in_sem.at[i])

time: 37 us -> 36.6 us (0.989)
  Pallas kernels: 36 us -> 35.6 us
    pallas_call x1, Pallas kernels: 36 us -> 35.6 us  [local(): pl.pallas_call(functools.partial(kernel, n_bank, n_lane, chunks), out_sha...]
where the time goes in v4:
time: 36.6 us; the launch traced here: 36.4 us
  Pallas kernels  35.6 us (97%)
  local copies, waits for them, and re-layouts  0.8 us (2%)
    pallas_call x1, Pallas kernels, local(): pl.pallas_call(functools.partial(kernel, n_bank, n_lane, chunks), out_sha...  35.6 us
    unnamed x1, local copies, waits for them, and re-layouts  0.8 us

profile of v4, /device:TPU:0, one launch (start us, length us, event | category | flops | bytes accessed | tf_op | source)
XLA Modules:
  0.0 36.4 jit_solution(9786338708769198908)
XLA Ops:
  0.0 35.6 %shard_map.46 = f32[2,4,128,128]{3,2,1,0:T(8,128)S(1)} custom-call(f32[2,4,128,128]{3,2,1,0:T(8,128)} %wave_hbm.1, f32[64,8,128]{2,1,0:T(8,128)} %bitcast.1, f32[2,128]{1,0:T(2,128)} %phase_hbm.1, f32[2,4]{1,0:T(2,128)} %mix_hbm.1), custom_call_target="tpu_custom_call" | custom-call | tf_op jit(solution)/shard_map/pallas_call | solution.py:252
  35.6 0.8 %copy.6 = f32[2,4,128,128]{3,2,1,0:T(8,128)} copy(f32[2,4,128,128]{3,2,1,0:T(8,128)S(1)} %shard_map.46) | data formatting | bytes 1048576
